TPU v7x, 8 devices: a whole 2x2x1 slice. The times are simulated.
8 devices in a mesh: pod: 1 (over z), dp: 2 (over y), tp: 4 (over x, core).
Axes of the slice: x: 2, y: 2, z: 1, core: 2. Of those that a mesh axis runs over, the one named last changes fastest.
Arguments:
- hidden: bfloat16 [2, 2048, 2304], P(('pod', 'dp'), 'tp')
- out_grad: bfloat16 [2, 2048, 2304], P(('pod', 'dp'), 'tp')
- gain_attn: float32 [2, 2304], replicated
- w_qkv: bfloat16 [2, 2304, 4, 1024], P(None, None, 'tp')
- w_out: bfloat16 [2, 2048, 2304], P(None, 'tp')
- gain_mlp: float32 [2, 2304], replicated
- w_gate: bfloat16 [2, 2304, 9216], P(None, None, 'tp')
- w_up: bfloat16 [2, 2304, 9216], P(None, None, 'tp')
- w_down: bfloat16 [2, 9216, 2304], P(None, 'tp')
Outputs:
- output 1: bfloat16 [2, 2048, 2304], P(('pod', 'dp'), 'tp')
- output 2: float32 [2, 2304], P('pod')
- output 3: bfloat16 [2, 2304, 4, 1024], P('pod', None, 'tp', 'dp')
- output 4: bfloat16 [2, 2048, 2304], P('pod', ('tp', 'dp'))
- output 5: float32 [2, 2304], P('pod')
- output 6: bfloat16 [2, 2304, 9216], P('pod', None, ('tp', 'dp'))
- output 7: bfloat16 [2, 2304, 9216], P('pod', None, ('tp', 'dp'))
- output 8: bfloat16 [2, 9216, 2304], P('pod', ('tp', 'dp'))
All inputs are finite; a program needn't handle non-finite values.
Results may differ from a plain program's by a relative error of at most 0.02.
Values are sent between devices in bfloat16 or wider.
A program may use at most 1 GiB of HBM per device.

v0:
```python
import jax
import jax.numpy as jnp
from jax import lax
from jax.sharding import PartitionSpec as P

NORM_EPS = 1e-5
MASK_FILL = -1e30
ACT_SPEC = P(('pod', 'dp'), 'tp', None)
IN_SPECS = (ACT_SPEC, ACT_SPEC, P(None, None), P(None, None, 'tp', None), P(None, 'tp', None), P(None, None), P(None, None, 'tp'), P(None, None, 'tp'), P(None, 'tp', None))
OUT_SPECS = (ACT_SPEC, P('pod', None), P('pod', None, 'tp', 'dp'), P('pod', ('tp', 'dp'), None), P('pod', None), P('pod', None, ('tp', 'dp')), P('pod', None, ('tp', 'dp')), P('pod', ('tp', 'dp'), None))


def rms_forward(values_in, gain_row):
    values_f = values_in.astype(jnp.float32)
    inv_rms = lax.rsqrt(jnp.mean(values_f * values_f, axis=-1, keepdims=True) + NORM_EPS)
    return (values_f * inv_rms * gain_row).astype(jnp.bfloat16), inv_rms


def rms_backward(grad_normed, values_in, inv_rms, gain_row):
    unit_rows = values_in.astype(jnp.float32) * inv_rms
    grad_unit = grad_normed * gain_row
    grad_values = inv_rms * (grad_unit - unit_rows * jnp.mean(grad_unit * unit_rows, axis=-1, keepdims=True))
    return grad_values, jnp.sum(grad_normed * unit_rows, axis=0)


def split_heads(qkv_rows, head_dim):
    seq_len, kv_local, group_cols = qkv_rows.shape
    group_size = group_cols // head_dim - 2
    grouped = qkv_rows.reshape(seq_len, kv_local, group_size + 2, head_dim)
    return grouped[:, :, :group_size], grouped[:, :, group_size], grouped[:, :, group_size + 1]


def causal_scores(query_rows, key_rows):
    seq_len = query_rows.shape[0]
    scores = jnp.einsum('sngd,tnd->ngst', query_rows, key_rows, preferred_element_type=jnp.float32) * query_rows.shape[-1] ** -0.5
    causal = lax.broadcasted_iota(jnp.int32, (seq_len, seq_len), 0) >= lax.broadcasted_iota(jnp.int32, (seq_len, seq_len), 1)
    return jnp.where(causal, scores, MASK_FILL)


def attention_forward(qkv_rows, head_dim):
    query_rows, key_rows, value_rows = split_heads(qkv_rows, head_dim)
    scores = causal_scores(query_rows, key_rows)
    row_max = jnp.max(scores, axis=-1, keepdims=True)
    log_sum = row_max + jnp.log(jnp.sum(jnp.exp(scores - row_max), axis=-1, keepdims=True))
    prob_bf = jnp.exp(scores - log_sum).astype(jnp.bfloat16)
    context = jnp.einsum('ngst,tnd->sngd', prob_bf, value_rows, preferred_element_type=jnp.float32)
    return context.astype(jnp.bfloat16), log_sum


def attention_backward(grad_ctx, qkv_rows, log_sum, head_dim):
    query_rows, key_rows, value_rows = split_heads(qkv_rows, head_dim)
    prob_f = jnp.exp(causal_scores(query_rows, key_rows) - log_sum)
    grad_value = jnp.einsum('ngst,sngd->tnd', prob_f.astype(jnp.bfloat16), grad_ctx, preferred_element_type=jnp.float32)
    grad_prob = jnp.einsum('sngd,tnd->ngst', grad_ctx, value_rows, preferred_element_type=jnp.float32)
    grad_score = prob_f * (grad_prob - jnp.sum(grad_prob * prob_f, axis=-1, keepdims=True)) * head_dim ** -0.5
    grad_score = grad_score.astype(jnp.bfloat16)
    grad_query = jnp.einsum('ngst,tnd->sngd', grad_score, key_rows, preferred_element_type=jnp.float32)
    grad_key = jnp.einsum('ngst,sngd->tnd', grad_score, query_rows, preferred_element_type=jnp.float32)
    grad_qkv = jnp.concatenate([grad_query, grad_key[:, :, None], grad_value[:, :, None]], axis=2)
    return grad_qkv.astype(jnp.bfloat16).reshape(qkv_rows.shape)


def mlp_forward(full_mlp, w_gate, w_up):
    gate_pre = jnp.dot(full_mlp, w_gate, preferred_element_type=jnp.float32)
    up_pre = jnp.dot(full_mlp, w_up, preferred_element_type=jnp.float32)
    return gate_pre, up_pre


def device_step(hidden, out_grad, gain_attn, w_qkv, w_out, gain_mlp, w_gate, w_up, w_down):
    layer_count, kv_local, group_cols = w_qkv.shape[0], w_qkv.shape[2], w_qkv.shape[3]
    head_dim = (group_cols - w_out.shape[1] // kv_local) // 2
    resid_rows = hidden[0]
    kept_state = []
    for layer_idx in range(layer_count):
        normed, inv_one = rms_forward(resid_rows, gain_attn[layer_idx])
        full_normed = lax.all_gather(normed, 'tp', axis=0, tiled=True)
        qkv_rows = jnp.einsum('sd,dnc->snc', full_normed, w_qkv[layer_idx], preferred_element_type=jnp.float32).astype(jnp.bfloat16)
        context, log_sum = attention_forward(qkv_rows, head_dim)
        attn_part = jnp.dot(context.reshape(qkv_rows.shape[0], -1), w_out[layer_idx], preferred_element_type=jnp.float32)
        attn_rows = lax.psum_scatter(attn_part, 'tp', scatter_dimension=0, tiled=True)
        mid_resid = (resid_rows.astype(jnp.float32) + attn_rows).astype(jnp.bfloat16)
        normed_mlp, inv_two = rms_forward(mid_resid, gain_mlp[layer_idx])
        kept_state.append((resid_rows, inv_one, normed, qkv_rows, context, log_sum, mid_resid, inv_two, normed_mlp))
        if layer_idx + 1 < layer_count:
            full_mlp = lax.all_gather(normed_mlp, 'tp', axis=0, tiled=True)
            gate_pre, up_pre = mlp_forward(full_mlp, w_gate[layer_idx], w_up[layer_idx])
            hidden_act = (jax.nn.silu(gate_pre) * up_pre).astype(jnp.bfloat16)
            mlp_part = jnp.dot(hidden_act, w_down[layer_idx], preferred_element_type=jnp.float32)
            mlp_rows = lax.psum_scatter(mlp_part, 'tp', scatter_dimension=0, tiled=True)
            resid_rows = (mid_resid.astype(jnp.float32) + mlp_rows).astype(jnp.bfloat16)
    grad_resid = out_grad[0]
    wqkv_grads, wout_grads, gate_grads, up_grads, down_grads, attn_gain_grads, mlp_gain_grads = [], [], [], [], [], [], []
    for layer_idx in reversed(range(layer_count)):
        resid_rows, inv_one, normed, qkv_rows, context, log_sum, mid_resid, inv_two, normed_mlp = kept_state[layer_idx]
        full_grad = lax.all_gather(grad_resid, 'tp', axis=0, tiled=True)
        full_mlp = lax.all_gather(normed_mlp, 'tp', axis=0, tiled=True)
        gate_pre, up_pre = mlp_forward(full_mlp, w_gate[layer_idx], w_up[layer_idx])
        gate_sig = jax.nn.sigmoid(gate_pre)
        gate_act = gate_pre * gate_sig
        hidden_act = (gate_act * up_pre).astype(jnp.bfloat16)
        grad_down = jnp.einsum('sf,sd->fd', hidden_act, full_grad, preferred_element_type=jnp.float32)
        grad_act = jnp.einsum('sd,fd->sf', full_grad, w_down[layer_idx], preferred_element_type=jnp.float32)
        grad_gate_pre = (grad_act * up_pre * gate_sig * (1.0 + gate_pre * (1.0 - gate_sig))).astype(jnp.bfloat16)
        grad_up_pre = (grad_act * gate_act).astype(jnp.bfloat16)
        grad_gate = jnp.einsum('sd,sf->df', full_mlp, grad_gate_pre, preferred_element_type=jnp.float32)
        grad_up = jnp.einsum('sd,sf->df', full_mlp, grad_up_pre, preferred_element_type=jnp.float32)
        grad_mlp_part = jnp.einsum('sf,df->sd', grad_gate_pre, w_gate[layer_idx], preferred_element_type=jnp.float32) + jnp.einsum('sf,df->sd', grad_up_pre, w_up[layer_idx], preferred_element_type=jnp.float32)
        grad_normed_mlp = lax.psum_scatter(grad_mlp_part, 'tp', scatter_dimension=0, tiled=True)
        grad_mid, gain_two_grad = rms_backward(grad_normed_mlp, mid_resid, inv_two, gain_mlp[layer_idx])
        grad_mid = (grad_mid + grad_resid.astype(jnp.float32)).astype(jnp.bfloat16)
        full_grad_mid = lax.all_gather(grad_mid, 'tp', axis=0, tiled=True)
        seq_len = full_grad_mid.shape[0]
        grad_wout = jnp.einsum('sh,sd->hd', context.reshape(seq_len, -1), full_grad_mid, preferred_element_type=jnp.float32)
        grad_ctx = jnp.einsum('sd,hd->sh', full_grad_mid, w_out[layer_idx], preferred_element_type=jnp.float32).astype(jnp.bfloat16).reshape(context.shape)
        grad_qkv = attention_backward(grad_ctx, qkv_rows, log_sum, head_dim)
        full_normed = lax.all_gather(normed, 'tp', axis=0, tiled=True)
        grad_wqkv = jnp.einsum('sd,snc->dnc', full_normed, grad_qkv, preferred_element_type=jnp.float32)
        grad_attn_part = jnp.einsum('snc,dnc->sd', grad_qkv, w_qkv[layer_idx], preferred_element_type=jnp.float32)
        grad_normed = lax.psum_scatter(grad_attn_part, 'tp', scatter_dimension=0, tiled=True)
        grad_in, gain_one_grad = rms_backward(grad_normed, resid_rows, inv_one, gain_attn[layer_idx])
        grad_resid = (grad_in + grad_mid.astype(jnp.float32)).astype(jnp.bfloat16)
        wqkv_grads.append(lax.psum_scatter(grad_wqkv, 'dp', scatter_dimension=2, tiled=True).astype(jnp.bfloat16))
        wout_grads.append(lax.psum_scatter(grad_wout, 'dp', scatter_dimension=0, tiled=True).astype(jnp.bfloat16))
        gate_grads.append(lax.psum_scatter(grad_gate, 'dp', scatter_dimension=1, tiled=True).astype(jnp.bfloat16))
        up_grads.append(lax.psum_scatter(grad_up, 'dp', scatter_dimension=1, tiled=True).astype(jnp.bfloat16))
        down_grads.append(lax.psum_scatter(grad_down, 'dp', scatter_dimension=0, tiled=True).astype(jnp.bfloat16))
        attn_gain_grads.append(gain_one_grad)
        mlp_gain_grads.append(gain_two_grad)
    gain_sums = lax.psum(jnp.stack([jnp.stack(attn_gain_grads[::-1]), jnp.stack(mlp_gain_grads[::-1])]), ('dp', 'tp'))
    return (grad_resid[None], gain_sums[0], jnp.stack(wqkv_grads[::-1]), jnp.stack(wout_grads[::-1]), gain_sums[1], jnp.stack(gate_grads[::-1]), jnp.stack(up_grads[::-1]), jnp.stack(down_grads[::-1]))


def solution(mesh):
    return jax.shard_map(device_step, mesh=mesh, in_specs=IN_SPECS, out_specs=OUT_SPECS, check_vma=False)
```

profile of v0, /device:TPU:0, one launch (start us, length us, event | category | flops | bytes accessed | tf_op | source)
XLA Modules:
  0.0 3839.0 jit_solution(7056816204371272154)
XLA Ops:
  19.4 60.6 %all-gather.10.cloned.1.call-done = bf16[2048,2304]{1,0:T(8,128)(2,1)} async-done(((bf16[512,2304]{1,0:T(8,128)(2,1)}), bf16[2048,2304]{1,0:T(8,128)(2,1)}) %all-gather.10.cloned.1.call-update) | async-done | bytes 9437200 | tf_op jit(solution)/shard_map/all_gather | solution.py:76
  156.6 130.3 %reduce-scatter.18.cloned.1.call-done = f32[512,2304]{1,0:T(8,128)} async-done(((f32[2048,2304]{1,0:T(8,128)}), f32[512,2304]{1,0:T(8,128)}) %reduce-scatter.18.cloned.1.call-update) | async-done | bytes 4718608 | tf_op jit(solution)/shard_map/reduce_scatter | solution.py:80
  293.5 61.9 %all-gather.12.cloned.1.call-done = bf16[2048,2304]{1,0:T(8,128)(2,1)} async-done(((bf16[512,2304]{1,0:T(8,128)(2,1)}), bf16[2048,2304]{1,0:T(8,128)(2,1)}) %all-gather.12.cloned.1.call-update) | async-done | bytes 9437200 | tf_op jit(solution)/shard_map/all_gather | solution.py:85
  385.8 35.3 multiply_convert_fusion.5
  451.5 131.5 %reduce-scatter.20.cloned.1.call-done = f32[512,2304]{1,0:T(8,128)} async-done(((f32[2048,2304]{1,0:T(8,128)}), f32[512,2304]{1,0:T(8,128)}) %reduce-scatter.20.cloned.1.call-update) | async-done | bytes 4718608 | tf_op jit(solution)/shard_map/reduce_scatter | solution.py:89
  589.7 61.9 %all-gather.14.cloned.1.call-done = bf16[2048,2304]{1,0:T(8,128)(2,1)} async-done(((bf16[512,2304]{1,0:T(8,128)(2,1)}), bf16[2048,2304]{1,0:T(8,128)(2,1)}) %all-gather.14.cloned.1.call-update) | async-done | bytes 9437200 | tf_op jit(solution)/shard_map/all_gather | solution.py:76
  727.2 131.5 %reduce-scatter.22.cloned.1.call-done = f32[512,2304]{1,0:T(8,128)} async-done(((f32[2048,2304]{1,0:T(8,128)}), f32[512,2304]{1,0:T(8,128)}) %reduce-scatter.22.cloned.1.call-update) | async-done | bytes 4718608 | tf_op jit(solution)/shard_map/reduce_scatter | solution.py:80
  866.0 61.1 %all-gather.16.cloned.1.call-done = bf16[2048,2304]{1,0:T(8,128)(2,1)} async-done(((bf16[512,2304]{1,0:T(8,128)(2,1)}), bf16[2048,2304]{1,0:T(8,128)(2,1)}) %all-gather.16.cloned.1.call-update) | async-done | bytes 9437200 | tf_op jit(solution)/shard_map/all_gather | solution.py:96
  927.2 31.6 fusion.20
  990.5 33.4 multiply_convert_fusion.3
  1054.3 30.9 convolution_add_fusion.1
  1085.7 131.1 %reduce-scatter.24.cloned.1.call-done = f32[512,2304]{1,0:T(8,128)} async-done(((f32[2048,2304]{1,0:T(8,128)}), f32[512,2304]{1,0:T(8,128)}) %reduce-scatter.24.cloned.1.call-update) | async-done | bytes 4718608 | tf_op jit(solution)/shard_map/reduce_scatter | solution.py:108
  1226.0 61.9 %all-gather.18.cloned.1.call-done = bf16[2048,2304]{1,0:T(8,128)(2,1)} async-done(((bf16[512,2304]{1,0:T(8,128)(2,1)}), bf16[2048,2304]{1,0:T(8,128)(2,1)}) %all-gather.18.cloned.1.call-update) | async-done | bytes 9437200 | tf_op jit(solution)/shard_map/all_gather | solution.py:111
  1406.8 131.3 %reduce-scatter.26.cloned.1.call-done = f32[512,2304]{1,0:T(8,128)} async-done(((f32[2048,2304]{1,0:T(8,128)}), f32[512,2304]{1,0:T(8,128)}) %reduce-scatter.26.cloned.1.call-update) | async-done | bytes 4718608 | tf_op jit(solution)/shard_map/reduce_scatter | solution.py:119
  1547.1 61.9 %all-gather.20.cloned.1.call-done = bf16[2048,2304]{1,0:T(8,128)(2,1)} async-done(((bf16[512,2304]{1,0:T(8,128)(2,1)}), bf16[2048,2304]{1,0:T(8,128)(2,1)}) %all-gather.20.cloned.1.call-update) | async-done | bytes 9437200 | tf_op jit(solution)/shard_map/all_gather | solution.py:95
  1609.0 33.4 multiply_convert_fusion.1
  1672.6 31.3 convolution_add_fusion
  1704.0 131.5 %reduce-scatter.28.cloned.1.call-done = f32[512,2304]{1,0:T(8,128)} async-done(((f32[2048,2304]{1,0:T(8,128)}), f32[512,2304]{1,0:T(8,128)}) %reduce-scatter.28.cloned.1.call-update) | async-done | bytes 4718608 | tf_op jit(solution)/shard_map/reduce_scatter | solution.py:108
  1844.6 33.6 fusion.39
  1878.3 30.7 fusion.150
  1909.0 30.8 fusion.148
  2029.4 30.7 fusion.147
  2218.0 161.3 %reduce-scatter.46.cloned.1.call-done = f32[2304,1152]{1,0:T(8,128)} async-done(((f32[2304,2304]{1,0:T(8,128)}), f32[2304,1152]{1,0:T(8,128)}) %reduce-scatter.46.cloned.1.call-update) | async-done | bytes 10616848 | tf_op jit(solution)/shard_map/reduce_scatter | solution.py:125
  2386.2 229.4 %reduce-scatter.42.cloned.1.call-done = f32[2304,1152]{1,0:T(8,128)} async-done(((f32[2304,2304]{1,0:T(8,128)}), f32[2304,1152]{1,0:T(8,128)}) %reduce-scatter.42.cloned.1.call-update) | async-done | bytes 10616848 | tf_op jit(solution)/shard_map/reduce_scatter | solution.py:124
  2622.4 53.1 %reduce-scatter.38.cloned.1.call-done = f32[256,2304]{1,0:T(8,128)} async-done(((f32[512,2304]{1,0:T(8,128)}), f32[256,2304]{1,0:T(8,128)}) %reduce-scatter.38.cloned.1.call-update) | async-done | bytes 2359312 | tf_op jit(solution)/shard_map/reduce_scatter | solution.py:123
  2677.3 108.8 %reduce-scatter.34.cloned.1.call-done = f32[2304,1,512]{2,0,1:T(8,128)} async-done(((f32[2304,1,1024]{2,0,1:T(8,128)}), f32[2304,1,512]{2,0,1:T(8,128)}) %reduce-scatter.34.cloned.1.call-update) | async-done | bytes 4718608 | tf_op jit(solution)/shard_map/reduce_scatter | solution.py:122
  2791.5 231.1 %reduce-scatter.48.cloned.1.call-done = f32[1152,2304]{1,0:T(8,128)} async-done(((f32[2304,2304]{1,0:T(8,128)}), f32[1152,2304]{1,0:T(8,128)}) %reduce-scatter.48.cloned.1.call-update) | async-done | bytes 10616848 | tf_op jit(solution)/shard_map/reduce_scatter | solution.py:126
  3034.4 224.7 %reduce-scatter.44.cloned.1.call-done = f32[2304,1152]{1,0:T(8,128)} async-done(((f32[2304,2304]{1,0:T(8,128)}), f32[2304,1152]{1,0:T(8,128)}) %reduce-scatter.44.cloned.1.call-update) | async-done | bytes 10616848 | tf_op jit(solution)/shard_map/reduce_scatter | solution.py:125
  3271.0 224.6 %reduce-scatter.40.cloned.1.call-done = f32[2304,1152]{1,0:T(8,128)} async-done(((f32[2304,2304]{1,0:T(8,128)}), f32[2304,1152]{1,0:T(8,128)}) %reduce-scatter.40.cloned.1.call-update) | async-done | bytes 10616848 | tf_op jit(solution)/shard_map/reduce_scatter | solution.py:124
  3507.8 47.3 %reduce-scatter.36.cloned.1.call-done = f32[256,2304]{1,0:T(8,128)} async-done(((f32[512,2304]{1,0:T(8,128)}), f32[256,2304]{1,0:T(8,128)}) %reduce-scatter.36.cloned.1.call-update) | async-done | bytes 2359312 | tf_op jit(solution)/shard_map/reduce_scatter | solution.py:123
  3558.6 106.5 %reduce-scatter.32.cloned.1.call-done = f32[2304,1,512]{2,0,1:T(8,128)} async-done(((f32[2304,1,1024]{2,0,1:T(8,128)}), f32[2304,1,512]{2,0,1:T(8,128)}) %reduce-scatter.32.cloned.1.call-update) | async-done | bytes 4718608 | tf_op jit(solution)/shard_map/reduce_scatter | solution.py:122
  3672.0 127.1 %reduce-scatter.30.cloned.1.call-done = f32[512,2304]{1,0:T(8,128)} async-done(((f32[2048,2304]{1,0:T(8,128)}), f32[512,2304]{1,0:T(8,128)}) %reduce-scatter.30.cloned.1.call-update) | async-done | bytes 4718608 | tf_op jit(solution)/shard_map/reduce_scatter | solution.py:119
  (246 shorter events, 831.7 us)
Async XLA Ops:
  7.2 72.8 %all-gather.10.cloned.1.call-start = ((), (), s32[]{:S(2)}) async-start(), calls=%async_computation.17 | async-start | bytes 11796480 | tf_op jit(solution)/shard_map/all_gather | solution.py:76
  15.2 271.7 %reduce-scatter.18.cloned.1.call-start = ((), (), s32[]{:S(2)}) async-start(), calls=%async_computation.18 | async-start | bytes 23592960 | tf_op jit(solution)/shard_map/reduce_scatter | solution.py:80
  155.3 200.1 %all-gather.12.cloned.1.call-start = ((), (), s32[]{:S(2)}) async-start(), calls=%async_computation.19 | async-start | bytes 11796480 | tf_op jit(solution)/shard_map/all_gather | solution.py:85
  156.6 229.1 %copy-start.21 = (f32[2304]{0:T(1024)}, f32[2304]{0:T(1024)S(1)}, u32[]{:S(2)}) copy-start(f32[2304]{0:T(1024)S(1)} %get-tuple-element.17) | copy-start | bytes 27652
  293.4 289.6 %reduce-scatter.20.cloned.1.call-start = ((), (), s32[]{:S(2)}) async-start(), calls=%async_computation.20 | async-start | bytes 23592960 | tf_op jit(solution)/shard_map/reduce_scatter | solution.py:89
  451.5 136.1 %copy-start.23 = (f32[2304]{0:T(1024)S(1)}, f32[2304]{0:T(1024)}, u32[]{:S(2)}) copy-start(f32[2304]{0:T(1024)} %get-tuple-element.18) | copy-start | bytes 27652
  451.5 200.1 %all-gather.14.cloned.1.call-start = ((), (), s32[]{:S(2)}) async-start(), calls=%async_computation.21 | async-start | bytes 11796480 | tf_op jit(solution)/shard_map/all_gather | solution.py:76
  589.6 269.1 %reduce-scatter.22.cloned.1.call-start = ((), (), s32[]{:S(2)}) async-start(), calls=%async_computation.22 | async-start | bytes 23592960 | tf_op jit(solution)/shard_map/reduce_scatter | solution.py:80
  727.1 200.0 %all-gather.16.cloned.1.call-start = ((), (), s32[]{:S(2)}) async-start(), calls=%async_computation.23 | async-start | bytes 11796480 | tf_op jit(solution)/shard_map/all_gather | solution.py:96
  865.2 125.3 %all-gather.24.cloned.1.call-start = ((), (), s32[]{:S(2)}) async-start(), calls=%async_computation.41 | async-start | bytes 11796480 | tf_op jit(solution)/shard_map/all_gather | solution.py:95
  866.0 350.9 %reduce-scatter.24.cloned.1.call-start = ((), (), s32[]{:S(2)}) async-start(), calls=%async_computation.24 | async-start | bytes 23592960 | tf_op jit(solution)/shard_map/reduce_scatter | solution.py:108
  1085.3 202.6 %all-gather.18.cloned.1.call-start = ((), (), s32[]{:S(2)}) async-start(), calls=%async_computation.25 | async-start | bytes 11796480 | tf_op jit(solution)/shard_map/all_gather | solution.py:111
  1225.9 312.2 %reduce-scatter.26.cloned.1.call-start = ((), (), s32[]{:S(2)}) async-start(), calls=%async_computation.26 | async-start | bytes 23592960 | tf_op jit(solution)/shard_map/reduce_scatter | solution.py:119
  1406.5 202.5 %all-gather.20.cloned.1.call-start = ((), (), s32[]{:S(2)}) async-start(), calls=%async_computation.27 | async-start | bytes 11796480 | tf_op jit(solution)/shard_map/all_gather | solution.py:95
  1547.1 288.5 %reduce-scatter.28.cloned.1.call-start = ((), (), s32[]{:S(2)}) async-start(), calls=%async_computation.28 | async-start | bytes 23592960 | tf_op jit(solution)/shard_map/reduce_scatter | solution.py:108
  1704.0 356.2 %all-gather.22.cloned.1.call-start = ((), (), s32[]{:S(2)}) async-start(), calls=%async_computation.29 | async-start | bytes 11796480 | tf_op jit(solution)/shard_map/all_gather | solution.py:111
  1844.5 366.6 %reduce-scatter.50.cloned.1.call-start = ((), (), s32[]{:S(2)}) async-start(), calls=%async_computation.40 | async-start | bytes 31850496 | tf_op jit(solution)/shard_map/reduce_scatter | solution.py:126
  1878.2 501.0 %reduce-scatter.46.cloned.1.call-start = ((), (), s32[]{:S(2)}) async-start(), calls=%async_computation.38 | async-start | bytes 31850496 | tf_op jit(solution)/shard_map/reduce_scatter | solution.py:125
  1909.0 706.7 %reduce-scatter.42.cloned.1.call-start = ((), (), s32[]{:S(2)}) async-start(), calls=%async_computation.36 | async-start | bytes 31850496 | tf_op jit(solution)/shard_map/reduce_scatter | solution.py:124
  1939.8 735.7 %reduce-scatter.38.cloned.1.call-start = ((), (), s32[]{:S(2)}) async-start(), calls=%async_computation.34 | async-start | bytes 7077888 | tf_op jit(solution)/shard_map/reduce_scatter | solution.py:123
  1951.7 834.4 %reduce-scatter.34.cloned.1.call-start = ((), (), s32[]{:S(2)}) async-start(), calls=%async_computation.32 | async-start | bytes 14155776 | tf_op jit(solution)/shard_map/reduce_scatter | solution.py:122
  1968.1 1054.5 %reduce-scatter.48.cloned.1.call-start = ((), (), s32[]{:S(2)}) async-start(), calls=%async_computation.39 | async-start | bytes 31850496 | tf_op jit(solution)/shard_map/reduce_scatter | solution.py:126
  1998.7 1260.4 %reduce-scatter.44.cloned.1.call-start = ((), (), s32[]{:S(2)}) async-start(), calls=%async_computation.37 | async-start | bytes 31850496 | tf_op jit(solution)/shard_map/reduce_scatter | solution.py:125
  2029.4 1466.3 %reduce-scatter.40.cloned.1.call-start = ((), (), s32[]{:S(2)}) async-start(), calls=%async_computation.35 | async-start | bytes 31850496 | tf_op jit(solution)/shard_map/reduce_scatter | solution.py:124
  2060.1 1495.0 %reduce-scatter.36.cloned.1.call-start = ((), (), s32[]{:S(2)}) async-start(), calls=%async_computation.33 | async-start | bytes 7077888 | tf_op jit(solution)/shard_map/reduce_scatter | solution.py:123
  2107.5 1557.6 %reduce-scatter.32.cloned.1.call-start = ((), (), s32[]{:S(2)}) async-start(), calls=%async_computation.31 | async-start | bytes 14155776 | tf_op jit(solution)/shard_map/reduce_scatter | solution.py:122
  2192.9 1606.2 %reduce-scatter.30.cloned.1.call-start = ((), (), s32[]{:S(2)}) async-start(), calls=%async_computation.30 | async-start | bytes 23592960 | tf_op jit(solution)/shard_map/reduce_scatter | solution.py:119
  2386.2 404.1 %copy-start.32 = (f32[2304]{0:T(1024)S(1)}, f32[2304]{0:T(1024)}, u32[]{:S(2)}) copy-start(f32[2304]{0:T(1024)} %get-tuple-element.10) | copy-start | bytes 27652
  2386.2 404.7 %copy-start.33 = (f32[2304]{0:T(1024)S(1)}, f32[2304]{0:T(1024)}, u32[]{:S(2)}) copy-start(f32[2304]{0:T(1024)} %get-tuple-element.12) | copy-start | bytes 27652
  3556.9 242.1 %copy-start.11 = (bf16[1,512,2304]{2,1,0:T(8,128)(2,1)S(1)}, bf16[1,512,2304]{2,1,0:T(8,128)(2,1)}, u32[]{:S(2)}) copy-start(bf16[1,512,2304]{2,1,0:T(8,128)(2,1)} %param.9) | copy-start | bytes 7077892
  3556.9 242.1 %copy-start.20 = (f32[2304]{0:T(1024)S(1)}, f32[2304]{0:T(1024)}, u32[]{:S(2)}) copy-start(f32[2304]{0:T(1024)} %copy-done.19) | copy-start | bytes 27652
  3557.0 242.1 %copy-start.38 = (f32[512]{0:T(512)S(1)}, f32[512]{0:T(512)}, u32[]{:S(2)}) copy-start(f32[512]{0:T(512)} %copy-done.37) | copy-start | bytes 6148
  (45 other events, 2399.0 us)
Sparse Core Ops, SparseCore 0:
  15.3 64.5 all-gather.9
  155.4 131.4 reduce-scatter.17
  293.6 61.7 all-gather.11
  451.6 131.4 reduce-scatter.19
  589.7 61.7 all-gather.13
  727.3 131.4 reduce-scatter.21
  865.4 61.7 all-gather.15
  928.7 61.7 all-gather.23
  1085.4 131.4 reduce-scatter.23
  1226.0 61.7 all-gather.17
  1406.6 131.4 reduce-scatter.25
  1547.2 61.7 all-gather.19
  1704.1 131.4 reduce-scatter.27
  1844.6 61.7 all-gather.21
  1908.6 234.2 reduce-scatter.49
  2145.0 234.2 reduce-scatter.45
  2381.4 234.2 reduce-scatter.41
  2618.3 57.1 reduce-scatter.37
  2678.4 107.7 reduce-scatter.33
  2788.3 234.2 reduce-scatter.47
  3024.8 234.2 reduce-scatter.43
  3261.4 234.2 reduce-scatter.39
  3497.9 57.1 reduce-scatter.35
  3557.3 107.7 reduce-scatter.31
  3667.6 131.4 reduce-scatter.29
where the time goes:
time: 3850 us; the launch traced here: 3840 us
  waiting for transfers between devices  2670 us (69%)
  matrix products  883 us (23%)
  other arithmetic  225 us (6%)
    reduce_scatter x2, waiting for transfers between devices, device_step(): lax.psum_scatter(grad_gate, 'dp', scatter_dimension=1, tiled=True)  454 us
    reduce_scatter x2, waiting for transfers between devices, device_step(): lax.psum_scatter(grad_up, 'dp', scatter_dimension=1, tiled=True)  386 us
    reduce_scatter x2, waiting for transfers between devices, device_step(): lax.psum_scatter(grad_mlp_part, 'tp', scatter_dimension=0, tiled=True)  263 us
    reduce_scatter x2, waiting for transfers between devices, device_step(): lax.psum_scatter(attn_part, 'tp', scatter_dimension=0, tiled=True)  262 us
    reduce_scatter x2, waiting for transfers between devices, device_step(): lax.psum_scatter(grad_attn_part, 'tp', scatter_dimension=0, tiled=True)  258 us
    reduce_scatter x2, waiting for transfers between devices, device_step(): lax.psum_scatter(grad_down, 'dp', scatter_dimension=0, tiled=True)  231 us
    reduce_scatter x2, waiting for transfers between devices, device_step(): lax.psum_scatter(grad_wqkv, 'dp', scatter_dimension=2, tiled=True)  215 us
    reduce_scatter x1, waiting for transfers between devices, device_step(): mlp_rows = lax.psum_scatter(mlp_part, 'tp', scatter_dimension=0, tiled=True)  132 us
  transfers between devices with their start and end apart: 25, of which 23 were waited for; matrix products, arithmetic and copies ran while one was open for 13% of the time, Pallas kernels for 0%

commit v1 on v0

v1 whole, which is shorter than its diff:
```python
import functools
import jax
import jax.numpy as jnp
from jax import lax
from jax.experimental import pallas as pl
from jax.experimental.pallas import tpu as pltpu
from jax.sharding import PartitionSpec as P


NORM_EPS = 1e-5
MASK_FILL = -1e30
BLOCK = 512
FWD_CHUNKS = 2
ACT_SPEC = P(('pod', 'dp'), 'tp', None)
IN_SPECS = (ACT_SPEC, ACT_SPEC, P(None, None), P(None, None, 'tp', None), P(None, 'tp', None), P(None, None), P(None, None, 'tp'), P(None, None, 'tp'), P(None, 'tp', None))
OUT_SPECS = (ACT_SPEC, P('pod', None), P('pod', None, 'tp', 'dp'), P('pod', ('tp', 'dp'), None), P('pod', None), P('pod', None, ('tp', 'dp')), P('pod', None, ('tp', 'dp')), P('pod', ('tp', 'dp'), None))

NN = (((1,), (0,)), ((), ()))
NT = (((1,), (1,)), ((), ()))
TN = (((0,), (0,)), ((), ()))


def mm(a, b, dims=NN):
    return lax.dot_general(a, b, dims, preferred_element_type=jnp.float32)


def rms_forward(values_in, gain_row):
    values_f = values_in.astype(jnp.float32)
    inv_rms = lax.rsqrt(jnp.mean(values_f * values_f, axis=-1, keepdims=True) + NORM_EPS)
    return (values_f * inv_rms * gain_row).astype(jnp.bfloat16), inv_rms


def rms_backward(grad_normed, values_in, inv_rms, gain_row):
    unit_rows = values_in.astype(jnp.float32) * inv_rms
    grad_unit = grad_normed * gain_row
    grad_values = inv_rms * (grad_unit - unit_rows * jnp.mean(grad_unit * unit_rows, axis=-1, keepdims=True))
    return grad_values, jnp.sum(grad_normed * unit_rows, axis=0)


def causal_fill(scores_t):
    keys = lax.broadcasted_iota(jnp.int32, scores_t.shape, 0)
    queries = lax.broadcasted_iota(jnp.int32, scores_t.shape, 1)
    return jnp.where(queries >= keys, scores_t, MASK_FILL)


def attention_forward_kernel(scale, q_ref, k_ref, v_ref, ctx_ref, lse_ref, vt_ref, s_ref):
    head, qi = pl.program_id(0), pl.program_id(1)

    @pl.when((head == 0) & (qi == 0))
    def _():
        vt_ref[...] = v_ref[...].T

    q = q_ref[...]

    def score(j, top, diagonal):
        rows = pl.ds(pl.multiple_of(j * BLOCK, BLOCK), BLOCK)
        s = mm(k_ref[rows, :], q, NT) * scale
        if diagonal:
            s = causal_fill(s)
        s_ref[rows, :] = s
        return jnp.maximum(top, jnp.max(s, axis=0, keepdims=True))

    top = lax.fori_loop(0, qi, lambda j, t: score(j, t, False), jnp.full((1, BLOCK), MASK_FILL, jnp.float32))
    top = score(qi, top, True)

    def expo(j, total):
        rows = pl.ds(pl.multiple_of(j * BLOCK, BLOCK), BLOCK)
        e = jnp.exp(s_ref[rows, :] - top)
        s_ref[rows, :] = e
        return total + jnp.sum(e, axis=0, keepdims=True)

    total = lax.fori_loop(0, qi + 1, expo, jnp.zeros((1, BLOCK), jnp.float32))
    inv_total = 1.0 / total

    def weigh(j, acc):
        rows = pl.ds(pl.multiple_of(j * BLOCK, BLOCK), BLOCK)
        p = (s_ref[rows, :] * inv_total).astype(jnp.bfloat16)
        return acc + mm(vt_ref[:, rows], p)

    acc = lax.fori_loop(0, qi + 1, weigh, jnp.zeros((vt_ref.shape[0], BLOCK), jnp.float32))
    ctx_ref[...] = acc.T.astype(jnp.bfloat16)
    lse_ref[0] = top + jnp.log(total)


def attention_forward(qkv_rows, head_dim):
    seq_len, cols = qkv_rows.shape
    heads = cols // head_dim - 2
    blocks = seq_len // BLOCK
    flops = 4 * heads * head_dim * seq_len * (seq_len + BLOCK) // 2
    return pl.pallas_call(
        functools.partial(attention_forward_kernel, head_dim ** -0.5),
        grid=(heads, blocks),
        in_specs=[pl.BlockSpec((BLOCK, head_dim), lambda h, i: (i, h)), pl.BlockSpec((seq_len, head_dim), lambda h, i: (0, heads)), pl.BlockSpec((seq_len, head_dim), lambda h, i: (0, heads + 1))],
        out_specs=[pl.BlockSpec((BLOCK, head_dim), lambda h, i: (i, h)), pl.BlockSpec((1, 1, BLOCK), lambda h, i: (h, 0, i))],
        out_shape=[jax.ShapeDtypeStruct((seq_len, heads * head_dim), jnp.bfloat16), jax.ShapeDtypeStruct((heads, 1, seq_len), jnp.float32)],
        scratch_shapes=[pltpu.VMEM((head_dim, seq_len), jnp.bfloat16), pltpu.VMEM((seq_len, BLOCK), jnp.float32)],
        compiler_params=pltpu.CompilerParams(dimension_semantics=('arbitrary', 'arbitrary'), vmem_limit_bytes=32 * 1024 * 1024),
        cost_estimate=pl.CostEstimate(flops=flops, bytes_accessed=6 * seq_len * head_dim * 2, transcendentals=heads * seq_len * seq_len // 2),
        name='attn_fwd',
    )(qkv_rows, qkv_rows, qkv_rows)


def attention_backward_kernel(scale, heads, q_ref, k_ref, v_ref, g_ref, lse_ref, out_ref, kt_ref, p_ref, dp_ref, dk_ref, dv_ref):
    head, qi = pl.program_id(0), pl.program_id(1)
    head_dim = q_ref.shape[1]

    @pl.when((head == 0) & (qi == 0))
    def _():
        kt_ref[...] = k_ref[...].T
        dk_ref[...] = jnp.zeros_like(dk_ref)
        dv_ref[...] = jnp.zeros_like(dv_ref)

    q, g, lse = q_ref[...], g_ref[...], lse_ref[0]

    def first(j, delta, diagonal):
        rows = pl.ds(pl.multiple_of(j * BLOCK, BLOCK), BLOCK)
        s = mm(k_ref[rows, :], q, NT) * scale
        if diagonal:
            s = causal_fill(s)
        p = jnp.exp(s - lse)
        dp = mm(v_ref[rows, :], g, NT)
        p_ref[rows, :] = p
        dp_ref[rows, :] = dp
        dv_ref[rows, :] += mm(p.astype(jnp.bfloat16), g)
        return delta + jnp.sum(p * dp, axis=0, keepdims=True)

    delta = lax.fori_loop(0, qi, lambda j, d: first(j, d, False), jnp.zeros((1, BLOCK), jnp.float32))
    delta = first(qi, delta, True)

    def second(j, acc):
        rows = pl.ds(pl.multiple_of(j * BLOCK, BLOCK), BLOCK)
        ds = (p_ref[rows, :] * (dp_ref[rows, :] - delta) * scale).astype(jnp.bfloat16)
        dk_ref[rows, :] += mm(ds, q)
        return acc + mm(kt_ref[:, rows], ds)

    acc = lax.fori_loop(0, qi + 1, second, jnp.zeros((head_dim, BLOCK), jnp.float32))
    rows = pl.ds(pl.multiple_of(qi * BLOCK, BLOCK), BLOCK)
    for h in range(heads):
        @pl.when(head == h)
        def _():
            out_ref[rows, h * head_dim:(h + 1) * head_dim] = acc.T.astype(jnp.bfloat16)

    @pl.when((head == heads - 1) & (qi == pl.num_programs(1) - 1))
    def _():
        out_ref[:, heads * head_dim:(heads + 1) * head_dim] = dk_ref[...].astype(jnp.bfloat16)
        out_ref[:, (heads + 1) * head_dim:] = dv_ref[...].astype(jnp.bfloat16)


def attention_backward(grad_ctx, qkv_rows, log_sum, head_dim):
    seq_len, cols = qkv_rows.shape
    heads = cols // head_dim - 2
    blocks = seq_len // BLOCK
    flops = 10 * heads * head_dim * seq_len * (seq_len + BLOCK) // 2
    return pl.pallas_call(
        functools.partial(attention_backward_kernel, head_dim ** -0.5, heads),
        grid=(heads, blocks),
        in_specs=[pl.BlockSpec((BLOCK, head_dim), lambda h, i: (i, h)), pl.BlockSpec((seq_len, head_dim), lambda h, i: (0, heads)), pl.BlockSpec((seq_len, head_dim), lambda h, i: (0, heads + 1)), pl.BlockSpec((BLOCK, head_dim), lambda h, i: (i, h)), pl.BlockSpec((1, 1, BLOCK), lambda h, i: (h, 0, i))],
        out_specs=pl.BlockSpec((seq_len, cols), lambda h, i: (0, 0)),
        out_shape=jax.ShapeDtypeStruct((seq_len, cols), jnp.bfloat16),
        scratch_shapes=[pltpu.VMEM((head_dim, seq_len), jnp.bfloat16), pltpu.VMEM((seq_len, BLOCK), jnp.float32), pltpu.VMEM((seq_len, BLOCK), jnp.float32), pltpu.VMEM((seq_len, head_dim), jnp.float32), pltpu.VMEM((seq_len, head_dim), jnp.float32)],
        compiler_params=pltpu.CompilerParams(dimension_semantics=('arbitrary', 'arbitrary'), vmem_limit_bytes=48 * 1024 * 1024),
        cost_estimate=pl.CostEstimate(flops=flops, bytes_accessed=12 * seq_len * head_dim * 2, transcendentals=heads * seq_len * seq_len // 2),
        name='attn_bwd',
    )(qkv_rows, qkv_rows, qkv_rows, grad_ctx, log_sum)


def gather_rows(values):
    return lax.all_gather(values, 'tp', axis=0, tiled=True)


def scatter_rows(values):
    return lax.psum_scatter(values, 'tp', scatter_dimension=0, tiled=True)


def tied(value, *after):
    return lax.optimization_barrier((value,) + after)[0]


def swap_dp(values):
    return lax.ppermute(values, 'dp', [(0, 1), (1, 0)])


def swap_tp(values, flip):
    return lax.ppermute(values, 'tp', [(i, i ^ flip) for i in range(lax.axis_size('tp'))])


def fetch_peer(chunks):
    mine = jnp.where(lax.axis_index('tp') % 2 == 0, chunks[0], chunks[1])
    first = swap_dp(mine)
    second = swap_tp(first, 1)
    return first, second


def dp_half(values, axis, index):
    size = values.shape[axis] // 2
    return lax.dynamic_slice_in_dim(values, index * size, size, axis=axis)


def layer_half(weights, layer, axis, index):
    sizes = list(weights.shape[1:])
    sizes[axis] //= 2
    starts = [layer, 0, 0]
    starts[1 + axis] = index * sizes[axis]
    return lax.dynamic_slice(weights, starts, [1] + sizes)[0]


def gate_parts(gate_pre, up_pre, grad_act):
    gate_sig = jax.nn.sigmoid(gate_pre)
    gate_act = gate_pre * gate_sig
    hidden_act = (gate_act * up_pre).astype(jnp.bfloat16)
    grad_gate_pre = (grad_act * up_pre * gate_sig * (1.0 + gate_pre * (1.0 - gate_sig))).astype(jnp.bfloat16)
    grad_up_pre = (grad_act * gate_act).astype(jnp.bfloat16)
    return hidden_act, grad_gate_pre, grad_up_pre


def gather_wout(shard, dp_me):
    mine = dp_half(shard, 0, dp_me)
    got = swap_tp(mine, 2)
    other = swap_dp(got)
    far = jnp.concatenate([jnp.where(dp_me == 0, got, other), jnp.where(dp_me == 0, other, got)], axis=0)
    near = jnp.concatenate([shard, far], axis=0)
    core = swap_tp(near, 1)
    return jnp.concatenate([near, core], axis=0)


def heads_to_rows(context):
    me, ways = lax.axis_index('tp'), lax.axis_size('tp')
    rows = context.shape[0] // ways
    pieces = []
    for flip in (0, 2, 1, 3):
        piece = lax.dynamic_slice_in_dim(context, (me ^ flip) * rows, rows, axis=0)
        pieces.append(swap_tp(piece, flip) if flip else piece)
    return jnp.concatenate(pieces, axis=1)


def replica_sum(values):
    for axis in ('dp', 'tp'):
        ways = lax.axis_size(axis)
        step = 1
        while step < ways:
            values = values + lax.ppermute(values, axis, [(i, i ^ step) for i in range(ways)])
            step *= 2
    return values


def row_chunks(values, count=2):
    return jnp.split(values, count, axis=0)


def device_step(hidden, out_grad, gain_attn, w_qkv, w_out, gain_mlp, w_gate, w_up, w_down):
    layer_count, kv_local, group_cols = w_qkv.shape[0], w_qkv.shape[2], w_qkv.shape[3]
    head_dim = (group_cols - w_out.shape[1] // kv_local) // 2
    w_qkv = w_qkv.reshape(layer_count, w_qkv.shape[1], kv_local * group_cols)
    dp_me = lax.axis_index('dp')
    resid_rows = hidden[0]
    kept_state = []
    full_wout = None
    for l in range(layer_count):
        normed, inv_one = rms_forward(resid_rows, gain_attn[l])
        full_normed = gather_rows(normed)
        if full_wout is None:
            full_wout = gather_wout(tied(w_out[l], full_normed), dp_me)
        qkv_rows = mm(full_normed, w_qkv[l]).astype(jnp.bfloat16)
        context, log_sum = attention_forward(qkv_rows, head_dim)
        attn_rows = mm(heads_to_rows(context), full_wout)
        mid_resid = (resid_rows.astype(jnp.float32) + attn_rows).astype(jnp.bfloat16)
        normed_mlp, inv_two = rms_forward(mid_resid, gain_mlp[l])
        kept_state.append((resid_rows, inv_one, normed, qkv_rows, context, log_sum, mid_resid, inv_two, normed_mlp))
        if l + 1 < layer_count:
            full_mlp = [gather_rows(rows) for rows in row_chunks(normed_mlp, FWD_CHUNKS)]
            full_wout = gather_wout(tied(w_out[l + 1], full_mlp[-1]), dp_me)
            scattered, part = [], None
            for rows in full_mlp:
                if part is not None:
                    rows = tied(rows, part)
                gate_pre = mm(rows, w_gate[l])
                up_pre = mm(rows, w_up[l])
                hidden_act = (jax.nn.silu(gate_pre) * up_pre).astype(jnp.bfloat16)
                part = mm(hidden_act, w_down[l])
                scattered.append(scatter_rows(part))
            resid_rows = (mid_resid.astype(jnp.float32) + jnp.concatenate(scattered, axis=0)).astype(jnp.bfloat16)
    grad_resid = out_grad[0]
    outs = {name: [None] * layer_count for name in ('qkv', 'out', 'gate', 'up', 'down', 'gain_one', 'gain_two')}
    after = None
    for l in reversed(range(layer_count)):
        resid_rows, inv_one, normed, qkv_rows, context, log_sum, mid_resid, inv_two, normed_mlp = kept_state[l]
        last = l + 1 == layer_count
        grad_parts = row_chunks(grad_resid)
        mlp_parts = row_chunks(normed_mlp if last else tied(normed_mlp, after))
        if last:
            grad_parts = [tied(rows, normed_mlp) for rows in grad_parts]
        mlp_rows, grad_rows = [], []
        for c in range(2):
            mlp_rows.append(gather_rows(mlp_parts[c]))
            grad_rows.append(gather_rows(grad_parts[c]))
        peer_grad = fetch_peer(grad_rows)
        peer_mlp = fetch_peer(mlp_rows)
        halves, scattered, part = [], [], None
        for c in range(2):
            rows = grad_rows[c] if part is None else tied(grad_rows[c], part)
            gate_pre = mm(mlp_rows[c], w_gate[l])
            up_pre = mm(mlp_rows[c], w_up[l])
            grad_act = mm(rows, w_down[l], NT)
            hidden_act, grad_gate_pre, grad_up_pre = gate_parts(gate_pre, up_pre, grad_act)
            part = mm(grad_gate_pre, w_gate[l], NT) + mm(grad_up_pre, w_up[l], NT)
            scattered.append(scatter_rows(tied(part, scattered[0]) if c else part))
            halves.append((hidden_act, grad_gate_pre, grad_up_pre))
        acts, gates, ups = zip(*halves)
        own_rows, own_grad = [tied(r, part) for r in mlp_rows], [tied(r, part) for r in grad_rows]
        sum_gate = sum(mm(r, dp_half(v, 1, dp_me), TN) for r, v in zip(own_rows, gates))
        sum_up = sum(mm(r, dp_half(v, 1, dp_me), TN) for r, v in zip(own_rows, ups))
        sum_down = sum(mm(dp_half(v, 1, dp_me), r, TN) for r, v in zip(own_grad, acts))
        gate_half, up_half, down_half = layer_half(w_gate, l, 1, dp_me), layer_half(w_up, l, 1, dp_me), layer_half(w_down, l, 0, dp_me)

        def peer_parts(m, g):
            gate_pre, up_pre = mm(m, gate_half), mm(m, up_half)
            grad_act = mm(g, down_half, NT)
            return gate_parts(gate_pre, up_pre, grad_act)

        scattered = tied(scattered, sum_gate, sum_up, sum_down)
        grad_mid, outs['gain_two'][l] = rms_backward(jnp.concatenate(scattered, axis=0), mid_resid, inv_two, gain_mlp[l])
        grad_mid = (grad_mid + grad_resid.astype(jnp.float32)).astype(jnp.bfloat16)
        full_grad_mid = gather_rows(grad_mid)
        first_mlp, first_grad = tied(peer_mlp[0], grad_mid), tied(peer_grad[0], grad_mid)
        first_values = peer_parts(first_mlp, first_grad)
        sum_down = sum_down + mm(first_values[0], tied(peer_grad[0], grad_mid), TN)
        full_grad_mid = tied(full_grad_mid, sum_down)
        their_wout = mm(dp_half(context, 1, 1 - dp_me), full_grad_mid, TN)
        got_wout = swap_dp(their_wout)
        grad_ctx = mm(full_grad_mid, w_out[l], NT).astype(jnp.bfloat16)
        grad_qkv = attention_backward(grad_ctx, qkv_rows, log_sum, head_dim)
        grad_attn_part = mm(grad_qkv, w_qkv[l], NT)
        grad_normed = scatter_rows(grad_attn_part)
        if not last:
            full_normed = gather_rows(tied(normed, full_grad_mid))
        full_normed, late_grad_mid, first_values, second_mlp, second_grad = tied((full_normed, full_grad_mid, first_values, peer_mlp[1], peer_grad[1]), grad_attn_part)
        their_wqkv = mm(full_normed, dp_half(grad_qkv, 1, 1 - dp_me), TN)
        got_wqkv = swap_dp(their_wqkv)
        my_wqkv = mm(full_normed, dp_half(grad_qkv, 1, dp_me), TN)
        my_wout = mm(dp_half(context, 1, dp_me), late_grad_mid, TN)
        after = my_wqkv
        first_values, second_mlp, second_grad = tied((first_values, second_mlp, second_grad), my_wqkv, my_wout)
        second_values = peer_parts(second_mlp, second_grad)
        outs['down'][l] = (sum_down + mm(second_values[0], peer_grad[1], TN)).astype(jnp.bfloat16)
        outs['gate'][l] = (sum_gate + sum(mm(r, v[1], TN) for r, v in zip(peer_mlp, (first_values, second_values)))).astype(jnp.bfloat16)
        outs['up'][l] = (sum_up + sum(mm(r, v[2], TN) for r, v in zip(peer_mlp, (first_values, second_values)))).astype(jnp.bfloat16)
        late = (outs['gate'][l], outs['up'][l], outs['down'][l])
        grad_normed = tied(grad_normed, *late)
        got_wout = tied(got_wout, *late)
        got_wqkv = tied(got_wqkv, *late)
        grad_in, outs['gain_one'][l] = rms_backward(grad_normed, resid_rows, inv_one, gain_attn[l])
        grad_resid = (grad_in + grad_mid.astype(jnp.float32)).astype(jnp.bfloat16)
        if last:
            got_wqkv = tied(got_wqkv, grad_resid)
            got_wout = tied(got_wout, grad_resid)
        outs['qkv'][l] = (my_wqkv + got_wqkv).astype(jnp.bfloat16).reshape(my_wqkv.shape[0], kv_local, -1)
        outs['out'][l] = (my_wout + got_wout).astype(jnp.bfloat16)
    gain_sums = replica_sum(jnp.stack([jnp.stack(outs['gain_one']), jnp.stack(outs['gain_two'])]))
    stacked = {name: jnp.stack(outs[name]) for name in ('qkv', 'out', 'gate', 'up', 'down')}
    return (grad_resid[None], gain_sums[0], stacked['qkv'], stacked['out'], gain_sums[1], stacked['gate'], stacked['up'], stacked['down'])


def solution(mesh):
    return jax.shard_map(device_step, mesh=mesh, in_specs=IN_SPECS, out_specs=OUT_SPECS, check_vma=False)
```

time: 3850 us -> 2380 us (0.62)
  waiting for transfers between devices: 2670 us -> 1010 us
  matrix products: 883 us -> 1090 us
  other arithmetic: 225 us -> 91.2 us
  Pallas kernels: 0 us -> 101 us
    reduce_scatter x17 -> x8, waiting for transfers between devices: 2300 us -> 95.2 us  [scatter_rows(): return lax.psum_scatter(values, 'tp', scatter_dimension=0, tiled=True)]
    ppermute x0 -> x27, waiting for transfers between devices: none -> 742 us  [the longest x10 593 us: swap_dp(): return lax.ppermute(values, 'dp', [(0, 1), (1, 0)])]
    dot_general x41 -> x76, matrix products: 883 us -> 1090 us  [mm(): return lax.dot_general(a, b, dims, preferred_element_type=jnp.float32)]
    all_gather x8 -> x15, waiting for transfers between devices: 372 us -> 173 us  [gather_rows(): return lax.all_gather(values, 'tp', axis=0, tiled=True)]
    pallas_call x0 -> x4, Pallas kernels: none -> 101 us  [the longest x2 60.5 us: attention_backward(): pl.pallas_call(functools.partial(attention_backward_kernel, head_dim ** (...]
    another operation x19 -> x10, other arithmetic: 133 us -> 37.4 us  [the longest x8 37.3 us: device_step(): jnp.stack(outs[name])]
  transfers between devices with their start and end apart: 25 -> 50, of which waited for: 23 -> 29; matrix products, arithmetic and copies ran while one was open for 13% -> 48% of each run, Pallas kernels for 0% -> 3%
where the time goes in v1:
time: 2380 us; the launch traced here: 2370 us
  matrix products  1090 us (46%)
  waiting for transfers between devices  1010 us (42%)
  Pallas kernels  101 us (4%)
  other arithmetic  91.2 us (4%)
  local copies, waits for them, and re-layouts  31.6 us (1%)
    dot_general x76, matrix products, mm(): return lax.dot_general(a, b, dims, preferred_element_type=jnp.float32)  1090 us
    ppermute x10, waiting for transfers between devices, swap_dp(): return lax.ppermute(values, 'dp', [(0, 1), (1, 0)])  593 us
    all_gather x15, waiting for transfers between devices, gather_rows(): return lax.all_gather(values, 'tp', axis=0, tiled=True)  173 us
    ppermute x14, waiting for transfers between devices, swap_tp(): lax.ppermute(values, 'tp', [(i, i ^ flip) for i in range(lax.axis_size('t...  147 us
    reduce_scatter x8, waiting for transfers between devices, scatter_rows(): return lax.psum_scatter(values, 'tp', scatter_dimension=0, tiled=True)  95.2 us
    pallas_call x2, Pallas kernels, attention_backward(): pl.pallas_call(functools.partial(attention_backward_kernel, head_dim ** (...  60.5 us
  transfers between devices with their start and end apart: 50, of which 29 were waited for; matrix products, arithmetic and copies ran while one was open for 48% of the time, Pallas kernels for 3%

profile of v1, /device:TPU:0, one launch (start us, length us, event | category | flops | bytes accessed | tf_op | source)
XLA Modules:
  0.0 2366.1 jit_solution(9466072961088273784)
XLA Ops:
  18.7 60.2 %all-gather.16.cloned.1.call-done = bf16[2048,2304]{1,0:T(8,128)(2,1)} async-done(((bf16[512,2304]{1,0:T(8,128)(2,1)}), bf16[2048,2304]{1,0:T(8,128)(2,1)}) %all-gather.16.cloned.1.call-update) | async-done | bytes 9437200 | tf_op jit(solution)/shard_map/all_gather | solution.py:168
  79.4 27.8 %collective-permute-done.3 = bf16[256,2304]{1,0:T(8,128)(2,1)S(1)} collective-permute-done((bf16[256,2304]{1,0:T(8,128)(2,1)S(1)}, bf16[256,2304]{1,0:T(8,128)(2,1)S(1)}, u32[]{:S(2)}, u32[]{:S(2)}) %collective-permute-start.3) | collective-permute-done | bytes 1179680 | tf_op jit(solution)/shard_map/ppermute | solution.py:184
  108.7 25.9 %collective-permute-done.4 = bf16[256,2304]{1,0:T(8,128)(2,1)} collective-permute-done((bf16[256,2304]{1,0:T(8,128)(2,1)S(1)}, bf16[256,2304]{1,0:T(8,128)(2,1)}, u32[]{:S(2)}, u32[]{:S(2)}) %collective-permute-start.4) | collective-permute-done | bytes 1179680 | tf_op jit(solution)/shard_map/ppermute | solution.py:180
  152.9 20.4 attn_fwd.2
  212.9 33.6 %all-gather.18.cloned.1.call-done = bf16[1024,2304]{1,0:T(8,128)(2,1)} async-done(((bf16[256,2304]{1,0:T(8,128)(2,1)}), bf16[1024,2304]{1,0:T(8,128)(2,1)}) %all-gather.18.cloned.1.call-update) | async-done | bytes 4718608 | tf_op jit(solution)/shard_map/all_gather | solution.py:168
  263.1 38.3 %fusion.36 = f32[1024,2304]{1,0:T(8,128)} fusion(bf16[2,2304,2304]{2,1,0:T(8,128)(2,1)} %param.17, f32[1024,2304]{1,0:T(8,128)} %fusion.48, bf16[1024,2304]{1,0:T(8,128)(2,1)} %all-gather.18.cloned.1.call-done, bf16[2,2304,2304]{2,1,0:T(8,128)(2,1)} %param.15), kind=kOutput, calls=%fused_computation.53 | convolution fusion | flops 21757427712 | bytes 44826624 | tf_op jit(solution)/shard_map/dot_general | solution.py:24
  301.6 17.6 fusion.46
  319.2 38.7 %fusion.34 = f32[1024,2304]{1,0:T(8,128)} fusion(bf16[2,2304,2304]{2,1,0:T(8,128)(2,1)} %param.17, f32[1024,2304]{1,0:T(8,128)} %fusion.46, bf16[1024,2304]{1,0:T(8,128)(2,1)} %all-gather.20.cloned.1.call-done, bf16[2,2304,2304]{2,1,0:T(8,128)(2,1)} %param.15), kind=kOutput, calls=%fused_computation.51 | convolution fusion | flops 21757427712 | bytes 44826624 | tf_op jit(solution)/shard_map/dot_general | solution.py:24
  373.9 75.4 %reduce-scatter.11.cloned.1.call-done = f32[256,2304]{1,0:T(8,128)} async-done(((f32[1024,2304]{1,0:T(8,128)}), f32[256,2304]{1,0:T(8,128)}) %reduce-scatter.11.cloned.1.call-update) | async-done | bytes 2359312 | tf_op jit(solution)/shard_map/reduce_scatter | solution.py:172
  456.6 47.2 %collective-permute-done.9 = bf16[256,2304]{1,0:T(8,128)(2,1)S(1)} collective-permute-done((bf16[256,2304]{1,0:T(8,128)(2,1)S(1)}, bf16[256,2304]{1,0:T(8,128)(2,1)S(1)}, u32[]{:S(2)}, u32[]{:S(2)}) %collective-permute-start.9) | collective-permute-done | bytes 1179680 | tf_op jit(solution)/shard_map/ppermute | solution.py:184
  505.2 22.7 collective-permute-done.10
  550.5 20.4 attn_fwd.3
  612.2 30.5 %all-gather.26.cloned.1.call-done = bf16[1024,2304]{1,0:T(8,128)(2,1)} async-done(((bf16[256,2304]{1,0:T(8,128)(2,1)}), bf16[1024,2304]{1,0:T(8,128)(2,1)}) %all-gather.26.cloned.1.call-update) | async-done | bytes 4718608 | tf_op jit(solution)/shard_map/all_gather | solution.py:168
  679.5 23.5 multiply_convert_fusion.6
  720.0 21.1 fusion.112
  751.8 17.7 fusion.20
  784.8 25.0 %multiply_convert_fusion.4 = (bf16[1024,2304]{1,0:T(8,128)(2,1)}, bf16[1024,2304]{1,0:T(8,128)(2,1)}, f32[1024,2304]{1,0:T(8,128)}) fusion(f32[1024,2304]{1,0:T(8,128)} %fusion.12, f32[1024,2304]{1,0:T(8,128)} %fusion.20, bf16[1024,2304]{1,0:T(8,128)(2,1)S(1)} %bitcast.276, bf16[2,2304,2304]{2,1,0:T(8,128)(2,1)} %param.17), kind=kOutput, calls=%fused_computation.103 | convolution fusion | flops 10902306816 | bytes 53084160 | tf_op jit(solution)/shard_map/dot_general | solution.py:24
  826.4 20.0 fusion.115
  934.8 99.2 %collective-permute-done.13 = bf16[1024,2304]{1,0:T(8,128)(2,1)} collective-permute-done((bf16[1024,2304]{1,0:T(8,128)(2,1)S(1)}, bf16[1024,2304]{1,0:T(8,128)(2,1)}, u32[]{:S(2)}, u32[]{:S(2)}) %collective-permute-start.13) | collective-permute-done | bytes 4718624 | tf_op jit(solution)/shard_map/ppermute | solution.py:180
  1034.0 99.7 %collective-permute-done.12 = bf16[1024,2304]{1,0:T(8,128)(2,1)S(1)} collective-permute-done((bf16[1024,2304]{1,0:T(8,128)(2,1)S(1)}, bf16[1024,2304]{1,0:T(8,128)(2,1)S(1)}, u32[]{:S(2)}, u32[]{:S(2)}) %collective-permute-start.12) | collective-permute-done | bytes 4718624 | tf_op jit(solution)/shard_map/ppermute | solution.py:180
  1193.0 30.3 %attn_bwd.2 = bf16[2048,1024]{1,0:T(8,128)(2,1)} custom-call(bf16[2048,1024]{1,0:T(8,128)(2,1)} %copy-done.6, bf16[2048,1024]{1,0:T(8,128)(2,1)} %copy-done.6, bf16[2048,1024]{1,0:T(8,128)(2,1)} %copy-done.6, bf16[2048,512]{1,0:T(8,128)(2,1)S(1)} %convolution_convert_fusion.1.g_ref, f32[2,1,2048]{2,1,0:T(1,128)S(1)} %get-tuple-element.87.lse_ref), custom_call_target="tpu_custom_call" | custom-call | flops 13421772800 | bytes 12582912 | tf_op jit(solution)/shard_map/attn_bwd/pallas_call | solution.py:154
  1359.8 19.3 fusion.9
  1430.1 20.0 all-gather.34.cloned.1.call-done
  1465.3 20.7 multiply_convert_fusion.3
  1503.0 19.7 fusion.118
  1557.1 23.6 multiply_convert_fusion.1
  1597.4 19.8 fusion.121
  1705.3 99.2 %collective-permute-done.17 = bf16[1024,2304]{1,0:T(8,128)(2,1)} collective-permute-done((bf16[1024,2304]{1,0:T(8,128)(2,1)S(1)}, bf16[1024,2304]{1,0:T(8,128)(2,1)}, u32[]{:S(2)}, u32[]{:S(2)}) %collective-permute-start.17) | collective-permute-done | bytes 4718624 | tf_op jit(solution)/shard_map/ppermute | solution.py:180
  1804.5 99.7 %collective-permute-done.16 = bf16[1024,2304]{1,0:T(8,128)(2,1)S(1)} collective-permute-done((bf16[1024,2304]{1,0:T(8,128)(2,1)S(1)}, bf16[1024,2304]{1,0:T(8,128)(2,1)S(1)}, u32[]{:S(2)}, u32[]{:S(2)}) %collective-permute-start.16) | collective-permute-done | bytes 4718624 | tf_op jit(solution)/shard_map/ppermute | solution.py:180
  1965.0 30.2 %attn_bwd.3 = bf16[2048,1024]{1,0:T(8,128)(2,1)} custom-call(bf16[2048,1024]{1,0:T(8,128)(2,1)} %copy-done.5, bf16[2048,1024]{1,0:T(8,128)(2,1)} %copy-done.5, bf16[2048,1024]{1,0:T(8,128)(2,1)} %copy-done.5, bf16[2048,512]{1,0:T(8,128)(2,1)S(1)} %convolution_convert_fusion.g_ref, f32[2,1,2048]{2,1,0:T(1,128)S(1)} %get-tuple-element.111.lse_ref), custom_call_target="tpu_custom_call" | custom-call | flops 13421772800 | bytes 12582912 | tf_op jit(solution)/shard_map/attn_bwd/pallas_call | solution.py:154
  2033.5 141.4 %collective-permute-done.26 = f32[256,2304]{1,0:T(8,128)S(1)} collective-permute-done((f32[256,2304]{1,0:T(8,128)S(1)}, f32[256,2304]{1,0:T(8,128)S(1)}, u32[]{:S(2)}, u32[]{:S(2)}) %collective-permute-start.26) | collective-permute-done | bytes 2359328 | tf_op jit(solution)/shard_map/ppermute | solution.py:180
  2292.9 19.4 fusion.7
  (483 shorter events, 1042.3 us)
Async XLA Ops:
  7.2 71.8 %all-gather.16.cloned.1.call-start = ((), (), s32[]{:S(2)}) async-start(), calls=%async_computation.8 | async-start | bytes 11796480 | tf_op jit(solution)/shard_map/all_gather | solution.py:168
  14.6 231.9 %all-gather.18.cloned.1.call-start = ((), (), s32[]{:S(2)}) async-start(), calls=%async_computation.9 | async-start | bytes 5898240 | tf_op jit(solution)/shard_map/all_gather | solution.py:168
  211.7 89.9 %all-gather.20.cloned.1.call-start = ((), (), s32[]{:S(2)}) async-start(), calls=%async_computation.11 | async-start | bytes 5898240 | tf_op jit(solution)/shard_map/all_gather | solution.py:168
  212.4 161.5 %reduce-scatter.9.cloned.1.call-start = ((), (), s32[]{:S(2)}) async-start(), calls=%async_computation.10 | async-start | bytes 11796480 | tf_op jit(solution)/shard_map/reduce_scatter | solution.py:172
  301.4 147.9 %reduce-scatter.11.cloned.1.call-start = ((), (), s32[]{:S(2)}) async-start(), calls=%async_computation.12 | async-start | bytes 11796480 | tf_op jit(solution)/shard_map/reduce_scatter | solution.py:172
  357.9 178.7 %all-gather.22.cloned.1.call-start = ((), (), s32[]{:S(2)}) async-start(), calls=%async_computation.13 | async-start | bytes 11796480 | tf_op jit(solution)/shard_map/all_gather | solution.py:168
  455.9 186.9 %all-gather.26.cloned.1.call-start = ((), (), s32[]{:S(2)}) async-start(), calls=%async_computation.15 | async-start | bytes 5898240 | tf_op jit(solution)/shard_map/all_gather | solution.py:168
  610.4 130.8 %all-gather.28.cloned.1.call-start = ((), (), s32[]{:S(2)}) async-start(), calls=%async_computation.17 | async-start | bytes 5898240 | tf_op jit(solution)/shard_map/all_gather | solution.py:168
  611.2 140.6 %all-gather.30.cloned.1.call-start = ((), (), s32[]{:S(2)}) async-start(), calls=%async_computation.18 | async-start | bytes 5898240 | tf_op jit(solution)/shard_map/all_gather | solution.py:168
  611.8 234.7 %reduce-scatter.13.cloned.1.call-start = ((), (), s32[]{:S(2)}) async-start(), calls=%async_computation.16 | async-start | bytes 11796480 | tf_op jit(solution)/shard_map/reduce_scatter | solution.py:172
  741.1 177.9 %reduce-scatter.15.cloned.1.call-start = ((), (), s32[]{:S(2)}) async-start(), calls=%async_computation.19 | async-start | bytes 11796480 | tf_op jit(solution)/shard_map/reduce_scatter | solution.py:172
  846.5 337.0 %all-gather.32.cloned.1.call-start = ((), (), s32[]{:S(2)}) async-start(), calls=%async_computation.20 | async-start | bytes 11796480 | tf_op jit(solution)/shard_map/all_gather | solution.py:168
  926.3 468.8 %reduce-scatter.17.cloned.1.call-start = ((), (), s32[]{:S(2)}) async-start(), calls=%async_computation.21 | async-start | bytes 23592960 | tf_op jit(solution)/shard_map/reduce_scatter | solution.py:172
  929.2 104.8 %collective-permute-start.13 = (bf16[1024,2304]{1,0:T(8,128)(2,1)S(1)}, bf16[1024,2304]{1,0:T(8,128)(2,1)}, u32[]{:S(2)}, u32[]{:S(2)}) collective-permute-start(bf16[1024,2304]{1,0:T(8,128)(2,1)S(1)} %broadcast_select_fusion.2), channel_id=1, source_target_pairs={{0,4},{4,0},{1,5},{5,1},{2,6},{6,2},{3,7},{7,3}} | collective-permute-start | bytes 14155784 | tf_op jit(solution)/shard_map/ppermute | solution.py:180
  934.3 199.4 %collective-permute-start.12 = (bf16[1024,2304]{1,0:T(8,128)(2,1)S(1)}, bf16[1024,2304]{1,0:T(8,128)(2,1)S(1)}, u32[]{:S(2)}, u32[]{:S(2)}) collective-permute-start(bf16[1024,2304]{1,0:T(8,128)(2,1)S(1)} %broadcast_select_fusion.3), channel_id=1, source_target_pairs={{0,4},{4,0},{1,5},{5,1},{2,6},{6,2},{3,7},{7,3}} | collective-permute-start | bytes 14155784 | tf_op jit(solution)/shard_map/ppermute | solution.py:180
  1238.6 174.8 %all-gather.36.cloned.1.call-start = ((), (), s32[]{:S(2)}) async-start(), calls=%async_computation.23 | async-start | bytes 5898240 | tf_op jit(solution)/shard_map/all_gather | solution.py:168
  1320.3 129.7 %all-gather.34.cloned.1.call-start = ((), (), s32[]{:S(2)}) async-start(), calls=%async_computation.22 | async-start | bytes 5898240 | tf_op jit(solution)/shard_map/all_gather | solution.py:168
  1404.2 118.5 %all-gather.40.cloned.1.call-start = ((), (), s32[]{:S(2)}) async-start(), calls=%async_computation.26 | async-start | bytes 5898240 | tf_op jit(solution)/shard_map/all_gather | solution.py:168
  1404.8 135.3 %all-gather.38.cloned.1.call-start = ((), (), s32[]{:S(2)}) async-start(), calls=%async_computation.25 | async-start | bytes 5898240 | tf_op jit(solution)/shard_map/all_gather | solution.py:168
  1430.0 187.2 %reduce-scatter.19.cloned.1.call-start = ((), (), s32[]{:S(2)}) async-start(), calls=%async_computation.24 | async-start | bytes 11796480 | tf_op jit(solution)/shard_map/reduce_scatter | solution.py:172
  1522.7 166.9 %reduce-scatter.21.cloned.1.call-start = ((), (), s32[]{:S(2)}) async-start(), calls=%async_computation.27 | async-start | bytes 11796480 | tf_op jit(solution)/shard_map/reduce_scatter | solution.py:172
  1617.2 337.3 %all-gather.42.cloned.1.call-start = ((), (), s32[]{:S(2)}) async-start(), calls=%async_computation.28 | async-start | bytes 11796480 | tf_op jit(solution)/shard_map/all_gather | solution.py:168
  1696.8 492.5 %all-gather.44.cloned.1.call-start = ((), (), s32[]{:S(2)}) async-start(), calls=%async_computation.30 | async-start | bytes 11796480 | tf_op jit(solution)/shard_map/all_gather | solution.py:168
  1699.7 104.8 %collective-permute-start.17 = (bf16[1024,2304]{1,0:T(8,128)(2,1)S(1)}, bf16[1024,2304]{1,0:T(8,128)(2,1)}, u32[]{:S(2)}, u32[]{:S(2)}) collective-permute-start(bf16[1024,2304]{1,0:T(8,128)(2,1)S(1)} %broadcast_select_fusion), channel_id=1, source_target_pairs={{0,4},{4,0},{1,5},{5,1},{2,6},{6,2},{3,7},{7,3}} | collective-permute-start | bytes 14155784 | tf_op jit(solution)/shard_map/ppermute | solution.py:180
  1704.8 199.4 %collective-permute-start.16 = (bf16[1024,2304]{1,0:T(8,128)(2,1)S(1)}, bf16[1024,2304]{1,0:T(8,128)(2,1)S(1)}, u32[]{:S(2)}, u32[]{:S(2)}) collective-permute-start(bf16[1024,2304]{1,0:T(8,128)(2,1)S(1)} %broadcast_select_fusion.1), channel_id=1, source_target_pairs={{0,4},{4,0},{1,5},{5,1},{2,6},{6,2},{3,7},{7,3}} | collective-permute-start | bytes 14155784 | tf_op jit(solution)/shard_map/ppermute | solution.py:180
  1954.5 390.4 %reduce-scatter.23.cloned.1.call-start = ((), (), s32[]{:S(2)}) async-start(), calls=%async_computation.29 | async-start | bytes 23592960 | tf_op jit(solution)/shard_map/reduce_scatter | solution.py:172
  2021.6 153.2 %collective-permute-start.24 = (f32[2304,512]{1,0:T(8,128)}, f32[2304,512]{1,0:T(8,128)}, u32[]{:S(2)}, u32[]{:S(2)}) collective-permute-start(f32[2304,512]{1,0:T(8,128)} %fusion.282), channel_id=1, source_target_pairs={{0,4},{4,0},{1,5},{5,1},{2,6},{6,2},{3,7},{7,3}} | collective-permute-start | bytes 14155784 | tf_op jit(solution)/shard_map/ppermute | solution.py:180
  2032.3 142.5 %collective-permute-start.26 = (f32[256,2304]{1,0:T(8,128)S(1)}, f32[256,2304]{1,0:T(8,128)S(1)}, u32[]{:S(2)}, u32[]{:S(2)}) collective-permute-start(f32[256,2304]{1,0:T(8,128)S(1)} %fusion.296), channel_id=1, source_target_pairs={{0,4},{4,0},{1,5},{5,1},{2,6},{6,2},{3,7},{7,3}} | collective-permute-start | bytes 7077896 | tf_op jit(solution)/shard_map/ppermute | solution.py:180
  2032.3 157.0 %collective-permute-start.18 = (bf16[1024,2304]{1,0:T(8,128)(2,1)}, bf16[1024,2304]{1,0:T(8,128)(2,1)}, u32[]{:S(2)}, u32[]{:S(2)}) collective-permute-start(bf16[1024,2304]{1,0:T(8,128)(2,1)} %copy-done.70), channel_id=1, source_target_pairs={{0,1},{1,0},{2,3},{3,2},{4,5},{5,4},{6,7},{7,6}} | collective-permute-start | bytes 14155784 | tf_op jit(solution)/shard_map/ppermute | solution.py:184
  2032.4 156.9 %collective-permute-start.19 = (bf16[1024,2304]{1,0:T(8,128)(2,1)}, bf16[1024,2304]{1,0:T(8,128)(2,1)}, u32[]{:S(2)}, u32[]{:S(2)}) collective-permute-start(bf16[1024,2304]{1,0:T(8,128)(2,1)} %collective-permute-done.17), channel_id=1, source_target_pairs={{0,1},{1,0},{2,3},{3,2},{4,5},{5,4},{6,7},{7,6}} | collective-permute-start | bytes 14155784 | tf_op jit(solution)/shard_map/ppermute | solution.py:184
  2187.7 124.5 %collective-permute-start.25 = (f32[256,2304]{1,0:T(8,128)}, f32[256,2304]{1,0:T(8,128)}, u32[]{:S(2)}, u32[]{:S(2)}) collective-permute-start(f32[256,2304]{1,0:T(8,128)} %fusion.298), channel_id=1, source_target_pairs={{0,4},{4,0},{1,5},{5,1},{2,6},{6,2},{3,7},{7,3}} | collective-permute-start | bytes 7077896 | tf_op jit(solution)/shard_map/ppermute | solution.py:180
  2210.8 129.5 %collective-permute-start.23 = (f32[2304,512]{1,0:T(8,128)}, f32[2304,512]{1,0:T(8,128)}, u32[]{:S(2)}, u32[]{:S(2)}) collective-permute-start(f32[2304,512]{1,0:T(8,128)} %fusion.284), channel_id=1, source_target_pairs={{0,4},{4,0},{1,5},{5,1},{2,6},{6,2},{3,7},{7,3}} | collective-permute-start | bytes 14155784 | tf_op jit(solution)/shard_map/ppermute | solution.py:180
  (134 other events, 3117.8 us)
Sparse Core Ops, SparseCore 0:
  14.7 64.2 all-gather.15
  211.8 34.6 all-gather.17
  248.6 34.6 all-gather.19
  301.5 72.3 reduce-scatter.8
  376.9 72.3 reduce-scatter.10
  456.0 80.5 all-gather.21
  608.0 34.6 all-gather.25
  644.8 34.6 all-gather.23
  681.0 34.6 all-gather.27
  717.1 34.6 all-gather.29
  754.9 72.3 reduce-scatter.12
  846.6 72.3 reduce-scatter.14
  926.5 61.4 all-gather.31
  1238.8 138.5 reduce-scatter.16
  1378.7 34.6 all-gather.35
  1415.4 34.6 all-gather.33
  1451.4 34.6 all-gather.39
  1487.5 34.6 all-gather.37
  1525.3 72.3 reduce-scatter.18
  1617.3 72.2 reduce-scatter.20
  1697.0 61.4 all-gather.41
  1954.7 61.4 all-gather.43
  2018.7 136.2 reduce-scatter.22
